TPU v7x, 512 devices: a whole 4x4x16 slice. The times are simulated.
512 devices in a mesh: row: 64 (over y, z), col: 8 (over x, core).
Axes of the slice: x: 4, y: 4, z: 16, core: 2. Of those that a mesh axis runs over, the one named last changes fastest.
Arguments:
- sources: bfloat16 [524288, 640], P(('row', 'col')), may hold values from -6 to 6
- tree_perm: int32 [524288], P(('row', 'col')), may hold values from 0 to 524287, as said below
- leaf_blocks: bfloat16 [524288, 512], P(('row', 'col')), may hold values from -0.25 to 0.25
- u_factors: bfloat16 [10, 32, 524288], P(None, None, ('row', 'col')), may hold values from -0.3125 to 0.3125
- v_factors: bfloat16 [10, 32, 524288], P(None, None, ('row', 'col')), as said below
- level_ranks: int32 [10], replicated, may hold values from 16 to 32
Outputs:
- products: bfloat16 [524288, 640], P(('row', 'col'))
Inputs may be any that keep to these rules, and one draw needn't show every extreme that they name: tree_perm is a permutation that maps each aligned block of 1024 positions onto the same block of initial indices. `v_factors`: entries of level l are of the order of the inverse square root of 524288 / 2^l.
All inputs are finite; a program needn't handle non-finite values.
Results may differ from a plain program's by a relative error of at most 0.0037.
Values sent between devices are 32-bit elements; how exact they have to be, the bound alone decides.
A program may use at most 64 MiB of HBM per device.

v0:
```python
import jax
import jax.numpy as jnp
from jax import lax
from jax.sharding import Mesh
from jax.sharding import PartitionSpec as P

COL = ("col_0", "col_1")
ROW_COL = ("row", "col_0", "col_1")


def partner(x, axis, distance):
    return lax.ppermute(x, axis, [(i, i ^ 1 << distance) for i in range(lax.axis_size(axis))])


def cut_rows(length, count):
    unit = 8 if length >= 8 * count else 1
    return [length // unit * k // count * unit for k in range(1, count)]


def stacked_from(x, axes, order):
    blocks = x
    for k in order:
        blocks = lax.all_gather(blocks, axes[k])
    done = order[::-1]
    back = [done.index(k) for k in range(len(axes))]
    blocks = blocks.transpose(*back, *range(len(axes), blocks.ndim))
    return blocks.reshape(-1, *x.shape)


def laid_out(blocks, dim):
    blocks = jnp.moveaxis(blocks, 0, dim)
    lengths = blocks.shape
    return blocks.reshape(*lengths[:dim], lengths[dim] * lengths[dim + 1], *lengths[dim + 2 :])


def gather_at_once(x, axes, dim):
    split_at = max(range(max(1, x.ndim - 1)), key=lambda d: x.shape[d])
    count, done = (len(axes), [])
    for first, share in enumerate(jnp.split(x, cut_rows(x.shape[split_at], count), axis=split_at)):
        if share.size:
            order = [(first - k) % count for k in range(count)]
            done.append(stacked_from(share, axes, order))
    return laid_out(jnp.concatenate(done, axis=split_at + 1), dim)


def per_device(sources, tree_perm, leaf_blocks, u_factors, v_factors, level_ranks):
    row_count, rhs_count = sources.shape
    leaf_size = leaf_blocks.shape[1]
    level_count, rank_cap, _ = u_factors.shape
    col_size = lax.axis_size(COL)
    col_bits = col_size.bit_length() - 1
    row_bits = lax.axis_size("row").bit_length() - 1
    dev_bits = row_bits + col_bits
    first_row = (lax.axis_index("row") * col_size + lax.axis_index(COL)) * row_count
    local_index = tree_perm - first_row
    ordered = sources[local_index]
    rank_mask = (lax.iota(jnp.int32, rank_cap)[None, :] < level_ranks[:, None]).astype(jnp.float32)
    partial_coef = jnp.einsum(
        "lkn,nr->lkr", v_factors[:dev_bits], ordered, preferred_element_type=jnp.float32
    )
    siblings = [None] * dev_bits
    running = partial_coef
    for bit_pos in range(col_bits):
        finish = dev_bits - 1 - bit_pos
        received = partner(running, COL, bit_pos)
        siblings[finish] = received[finish]
        running = running[:finish] + received[:finish]
    share_width = rhs_count // col_size
    running = lax.dynamic_slice_in_dim(running, lax.axis_index(COL) * share_width, share_width, 2)
    coarse = [None] * row_bits
    for bit_pos in range(row_bits):
        finish = row_bits - 1 - bit_pos
        received = partner(running, "row", bit_pos)
        coarse[finish] = received[finish]
        running = running[:finish] + received[:finish]
    coarse_stack = jnp.stack(coarse)
    coarse_stack = gather_at_once(coarse_stack, COL, 2)
    far_coef = (
        jnp.concatenate([coarse_stack, jnp.stack(siblings[row_bits:])], axis=0)
        * rank_mask[:dev_bits, :, None]
    ).astype(jnp.bfloat16)
    leaf_count = row_count // leaf_size
    result = jnp.einsum(
        "gij,gjr->gir",
        leaf_blocks.reshape(leaf_count, leaf_size, leaf_size),
        ordered.reshape(leaf_count, leaf_size, rhs_count),
        preferred_element_type=jnp.float32,
    ).reshape(row_count, rhs_count)
    result = result + jnp.einsum(
        "lkn,lkr->nr", u_factors[:dev_bits], far_coef, preferred_element_type=jnp.float32
    )
    cluster_rows = row_count >> 9 - dev_bits + 1
    groups = row_count // cluster_rows
    near_coef = jnp.einsum(
        "kgs,gsr->gkr",
        v_factors[9].reshape(rank_cap, groups, cluster_rows),
        ordered.reshape(groups, cluster_rows, rhs_count),
        preferred_element_type=jnp.float32,
    )
    near_coef = near_coef.reshape(groups // 2, 2, rank_cap, rhs_count)[:, ::-1].reshape(
        groups, rank_cap, rhs_count
    )
    near_coef = (near_coef * rank_mask[9][None, :, None]).astype(jnp.bfloat16)
    result = result + jnp.einsum(
        "kgs,gkr->gsr",
        u_factors[9].reshape(rank_cap, groups, cluster_rows),
        near_coef,
        preferred_element_type=jnp.float32,
    ).reshape(row_count, rhs_count)
    return jnp.zeros_like(sources).at[local_index].set(result.astype(jnp.bfloat16))


def solution(mesh):
    torus = Mesh(mesh.devices.reshape(mesh.shape["row"], 4, 2), ("row", "col_0", "col_1"))
    placed = (
        P(ROW_COL, None),
        P(ROW_COL),
        P(ROW_COL, None),
        P(None, None, ROW_COL),
        P(None, None, ROW_COL),
        P(),
    )
    return jax.shard_map(
        per_device, mesh=torus, in_specs=placed, out_specs=P(ROW_COL, None), check_vma=False
    )
```

profile of v0, /device:TPU:1, one launch (start us, length us, event | category | flops | bytes accessed | tf_op | source)
XLA Modules:
  0.0 154.2 jit_solution(17403796162434309323)
XLA Ops:
  1.3 4.0 %gather_fusion = bf16[1024,640]{1,0:T(8,128)(2,1)S(1)} fusion(bf16[1024,640]{1,0:T(8,128)(2,1)S(1)} %copy-done, s32[1024]{0:T(1024)S(1)} %get-tuple-element.5), kind=kCustom, calls=%fused_computation | custom fusion | bytes 2625536 | tf_op jit(solution)/shard_map/gather | solution.py:56
  6.0 8.7 %collective-permute-start = (f32[9,32,640]{2,1,0:T(8,128)S(1)}, f32[9,32,640]{2,1,0:T(8,128)S(1)}, u32[]{:S(2)}, u32[]{:S(2)}) collective-permute-start(f32[9,32,640]{2,1,0:T(8,128)S(1)} %fusion.4), channel_id=1, source_target_pairs={{0,1},{1,0},{2,3},{3,2},{4,5},{5,4},{6,7},{7,6},{8,9},{9,8},{10,11... | collective-permute-start | bytes 2211848 | tf_op jit(solution)/shard_map/ppermute | solution.py:12
  16.7 1.9 %collective-permute-start.1 = (f32[8,32,640]{2,1,0:T(8,128)S(1)}, f32[8,32,640]{2,1,0:T(8,128)S(1)}, u32[]{:S(2)}, u32[]{:S(2)}) collective-permute-start(f32[8,32,640]{2,1,0:T(8,128)S(1)} %slice_add_fusion), channel_id=1, source_target_pairs={{0,2},{1,3},{2,0},{3,1},{4,6},{5,7},{6,4},{7,5},{8,10},{9,11},{10,... | collective-permute-start | bytes 1966088 | tf_op jit(solution)/shard_map/ppermute | solution.py:12
  18.6 15.9 %collective-permute-done.1 = f32[8,32,640]{2,1,0:T(8,128)S(1)} collective-permute-done((f32[8,32,640]{2,1,0:T(8,128)S(1)}, f32[8,32,640]{2,1,0:T(8,128)S(1)}, u32[]{:S(2)}, u32[]{:S(2)}) %collective-permute-start.1) | collective-permute-done | bytes 655392 | tf_op jit(solution)/shard_map/ppermute | solution.py:12
  37.3 14.8 %collective-permute-done.2 = f32[7,32,640]{2,1,0:T(8,128)} collective-permute-done((f32[7,32,640]{2,1,0:T(8,128)S(1)}, f32[7,32,640]{2,1,0:T(8,128)}, u32[]{:S(2)}, u32[]{:S(2)}) %collective-permute-start.2) | collective-permute-done | bytes 573472 | tf_op jit(solution)/shard_map/ppermute | solution.py:12
  53.4 1.9 %collective-permute-start.3 = (f32[6,32,80]{2,1,0:T(8,128)S(1)}, f32[6,32,80]{2,1,0:T(8,128)S(1)}, u32[]{:S(2)}, u32[]{:S(2)}) collective-permute-start(f32[6,32,80]{2,1,0:T(8,128)S(1)} %dynamic-slice_add_fusion), channel_id=1, source_target_pairs={{0,8},{8,0},{16,24},{24,16},{32,40},{40,32},{48,56},{56,48},{64,72... | collective-permute-start | bytes 184328 | tf_op jit(solution)/shard_map/ppermute | solution.py:12
  55.3 2.5 %fusion.20 = f32[2,640,512]{1,2,0:T(8,128)} fusion(bf16[2,512,512]{2,1,0:T(8,128)(2,1)S(1)} %bitcast.49, bf16[2,512,640]{2,1,0:T(8,128)(2,1)S(1)} %bitcast.43), kind=kOutput, calls=%fused_computation.42 | convolution fusion | flops 671088640 | bytes 4980736 | tf_op jit(solution)/shard_map/gij,gjr->gir/dot_general | solution.py:83
  58.7 1.9 %collective-permute-start.4 = (f32[5,32,80]{2,1,0:T(8,128)S(1)}, f32[5,32,80]{2,1,0:T(8,128)S(1)}, u32[]{:S(2)}, u32[]{:S(2)}) collective-permute-start(f32[5,32,80]{2,1,0:T(8,128)S(1)} %slice_add_fusion.2), channel_id=1, source_target_pairs={{0,16},{8,24},{16,0},{24,8},{32,48},{40,56},{48,32},{56,40},{64,80... | collective-permute-start | bytes 153608 | tf_op jit(solution)/shard_map/ppermute | solution.py:12
  61.0 4.7 %collective-permute-done.4 = f32[5,32,80]{2,1,0:T(8,128)S(1)} collective-permute-done((f32[5,32,80]{2,1,0:T(8,128)S(1)}, f32[5,32,80]{2,1,0:T(8,128)S(1)}, u32[]{:S(2)}, u32[]{:S(2)}) %collective-permute-start.4) | collective-permute-done | bytes 51232 | tf_op jit(solution)/shard_map/ppermute | solution.py:12
  65.7 4.9 %collective-permute-start.5 = (f32[4,32,80]{2,1,0:T(8,128)S(1)}, f32[4,32,80]{2,1,0:T(8,128)S(1)}, u32[]{:S(2)}, u32[]{:S(2)}) collective-permute-start(f32[4,32,80]{2,1,0:T(8,128)S(1)} %slice_add_fusion.3), channel_id=1, source_target_pairs={{0,32},{8,40},{16,48},{24,56},{32,0},{40,8},{48,16},{56,24},{64,96... | collective-permute-start | bytes 122888 | tf_op jit(solution)/shard_map/ppermute | solution.py:12
  70.8 5.3 %collective-permute-done.5 = f32[4,32,80]{2,1,0:T(8,128)S(1)} collective-permute-done((f32[4,32,80]{2,1,0:T(8,128)S(1)}, f32[4,32,80]{2,1,0:T(8,128)S(1)}, u32[]{:S(2)}, u32[]{:S(2)}) %collective-permute-start.5) | collective-permute-done | bytes 40992 | tf_op jit(solution)/shard_map/ppermute | solution.py:12
  76.0 10.5 %collective-permute-start.6 = (f32[3,32,80]{2,1,0:T(8,128)S(1)}, f32[3,32,80]{2,1,0:T(8,128)S(1)}, u32[]{:S(2)}, u32[]{:S(2)}) collective-permute-start(f32[3,32,80]{2,1,0:T(8,128)S(1)} %slice_add_fusion.4), channel_id=1, source_target_pairs={{0,64},{8,72},{16,80},{24,88},{32,96},{40,104},{48,112},{56,120},{... | collective-permute-start | bytes 92168 | tf_op jit(solution)/shard_map/ppermute | solution.py:12
  86.6 3.0 %collective-permute-done.6 = f32[3,32,80]{2,1,0:T(8,128)S(1)} collective-permute-done((f32[3,32,80]{2,1,0:T(8,128)S(1)}, f32[3,32,80]{2,1,0:T(8,128)S(1)}, u32[]{:S(2)}, u32[]{:S(2)}) %collective-permute-start.6) | collective-permute-done | bytes 30752 | tf_op jit(solution)/shard_map/ppermute | solution.py:12
  91.6 2.9 %collective-permute-done.7 = f32[2,32,80]{2,1,0:T(8,128)S(1)} collective-permute-done((f32[2,32,80]{2,1,0:T(8,128)S(1)}, f32[2,32,80]{2,1,0:T(8,128)S(1)}, u32[]{:S(2)}, u32[]{:S(2)}) %collective-permute-start.7) | collective-permute-done | bytes 20512 | tf_op jit(solution)/shard_map/ppermute | solution.py:12
  94.5 3.2 %collective-permute-start.8 = (f32[1,32,80]{2,1,0:T(8,128)S(1)}, f32[1,32,80]{2,1,0:T(8,128)S(1)}, u32[]{:S(2)}, u32[]{:S(2)}) collective-permute-start(f32[1,32,80]{2,1,0:T(8,128)S(1)} %slice_add_fusion.6), channel_id=1, source_target_pairs={{0,256},{8,264},{16,272},{24,280},{32,288},{40,296},{48,304},{56,3... | collective-permute-start | bytes 30728 | tf_op jit(solution)/shard_map/ppermute | solution.py:12
  97.8 2.0 %fusion.14 = f32[2,640,512]{1,2,0:T(8,128)} fusion(bf16[2,32,640]{2,1,0:T(8,128)(2,1)S(1)} %multiply_convert_fusion, bf16[32,2,512]{2,1,0:T(2,128)(2,1)S(1)} %reshape_squeeze.7), kind=kOutput, calls=%fused_computation.23 | convolution fusion | flops 41943040 | bytes 2768896 | tf_op jit(solution)/shard_map/kgs,gkr->gsr/dot_general | solution.py:104
  99.8 3.2 %copy.29 = f32[1024,640]{0,1:T(8,128)} copy(f32[1024,640]{1,0:T(8,128)} %bitcast.46) | data formatting | bytes 5242880 | tf_op jit(solution)/shard_map/reshape | solution.py:109
  103.1 3.2 %copy.24 = f32[1024,640]{0,1:T(8,128)} copy(f32[1024,640]{1,0:T(8,128)} %bitcast.45) | data formatting | bytes 5242880 | tf_op jit(solution)/shard_map/reshape | solution.py:88
  107.3 9.1 %all-gather.2 = f32[12,16,80]{2,1,0:T(8,128)S(1)} all-gather(f32[6,16,80]{2,1,0:T(8,128)S(1)} %get-tuple-element.8), channel_id=4, replica_groups=mesh['row'=64,'col_0'=4,'col_1'=2] {'col_1'}, dimensions={0}, use_global_device_ids=true | all-gather | bytes 92160 | tf_op jit(solution)/shard_map/all_gather | solution.py:23
  116.4 10.0 %all-gather = f32[24,16,80]{2,1,0:T(8,128)S(1)} all-gather(f32[6,16,80]{2,1,0:T(8,128)S(1)} %get-tuple-element.7), channel_id=2, replica_groups=mesh['row'=64,'col_0'=4,'col_1'=2] {'col_0'}, dimensions={0}, use_global_device_ids=true | all-gather | bytes 153600 | tf_op jit(solution)/shard_map/all_gather | solution.py:23
  126.4 4.5 %all-gather.1 = f32[8,6,16,80]{3,2,1,0:T(8,128)S(1)} all-gather(f32[4,6,16,80]{3,2,1,0:T(8,128)S(1)} %bitcast.50), channel_id=3, replica_groups=mesh['row'=64,'col_0'=4,'col_1'=2] {'col_1'}, dimensions={0}, use_global_device_ids=true | all-gather | bytes 368640 | tf_op jit(solution)/shard_map/all_gather | solution.py:23
  130.9 10.3 %all-gather.3 = f32[8,6,16,80]{3,2,1,0:T(8,128)S(1)} all-gather(f32[2,6,16,80]{3,2,1,0:T(8,128)S(1)} %bitcast.51), channel_id=5, replica_groups=mesh['row'=64,'col_0'=4,'col_1'=2] {'col_0'}, dimensions={0}, use_global_device_ids=true | all-gather | bytes 307200 | tf_op jit(solution)/shard_map/all_gather | solution.py:23
  142.3 3.7 %fusion.1 = bf16[1024,640]{0,1:T(8,128)(2,1)S(1)} fusion(f32[1024,640]{0,1:T(8,128)} %copy.29, f32[1024,640]{0,1:T(8,128)} %copy.24, bf16[10,32,1024]{2,1,0:T(8,128)(2,1)} %param.9, f32[1,32,640]{2,1,0:T(8,128)S(1)} %slice-done, f32[1,32,640]{2,1,0:T(8,128)S(1)} %slice-done.1, f32[1,32,640]{2,1,0:T(8,128)S(1)} %slice.143, f32[6,32,640]{2,1,0:T(8,128)S(1)} %reshape.36, ...), kind=kOutput, calls=%fused_computation.4 | convolution fusion | flops 380375040 | bytes 7881856 | tf_op jit(solution)/shard_map/lkn,lkr->nr/dot_general | solution.py:89
  147.4 6.8 %scatter_custom_fusion = bf16[1024,640]{1,0:T(8,128)(2,1)} fusion(s32[1024]{0:T(1024)S(1)} %get-tuple-element.6, bf16[1024,640]{1,0:T(8,128)(2,1)} %copy.28, bf16[]{:T(256)} %constant.10.clone.1), kind=kCustom, calls=%fused_computation.13 | custom fusion | bytes 1311232 | tf_op jit(solution)/shard_map/scatter | solution.py:110
  (56 shorter events, 14.6 us)
Async XLA Ops:
  0.0 1.3 copy-start
  1.3 4.0 %copy-start.4 = (bf16[10,32,1024]{2,1,0:T(8,128)(2,1)S(1)}, bf16[10,32,1024]{2,1,0:T(8,128)(2,1)}, u32[]{:S(2)}) copy-start(bf16[10,32,1024]{2,1,0:T(8,128)(2,1)} %param.10) | copy-start | bytes 1966084
  6.0 10.6 %collective-permute-start = (f32[9,32,640]{2,1,0:T(8,128)S(1)}, f32[9,32,640]{2,1,0:T(8,128)S(1)}, u32[]{:S(2)}, u32[]{:S(2)}) collective-permute-start(f32[9,32,640]{2,1,0:T(8,128)S(1)} %fusion.4), channel_id=1, source_target_pairs={{0,1},{1,0},{2,3},{3,2},{4,5},{5,4},{6,7},{7,6},{8,9},{9,8},{10,11... | collective-permute-start | bytes 2211848 | tf_op jit(solution)/shard_map/ppermute | solution.py:12
  16.6 18.0 %copy-start.2 = (f32[9,32,640]{2,1,0:T(8,128)}, f32[9,32,640]{2,1,0:T(8,128)S(1)}, u32[]{:S(2)}) copy-start(f32[9,32,640]{2,1,0:T(8,128)S(1)} %collective-permute-done) | copy-start | bytes 2211844
  16.7 17.8 %collective-permute-start.1 = (f32[8,32,640]{2,1,0:T(8,128)S(1)}, f32[8,32,640]{2,1,0:T(8,128)S(1)}, u32[]{:S(2)}, u32[]{:S(2)}) collective-permute-start(f32[8,32,640]{2,1,0:T(8,128)S(1)} %slice_add_fusion), channel_id=1, source_target_pairs={{0,2},{1,3},{2,0},{3,1},{4,6},{5,7},{6,4},{7,5},{8,10},{9,11},{10,... | collective-permute-start | bytes 1966088 | tf_op jit(solution)/shard_map/ppermute | solution.py:12
  34.5 0.9 copy-start.3
  35.4 16.8 %collective-permute-start.2 = (f32[7,32,640]{2,1,0:T(8,128)S(1)}, f32[7,32,640]{2,1,0:T(8,128)}, u32[]{:S(2)}, u32[]{:S(2)}) collective-permute-start(f32[7,32,640]{2,1,0:T(8,128)S(1)} %slice_add_fusion.1), channel_id=1, source_target_pairs={{0,4},{1,5},{2,6},{3,7},{4,0},{5,1},{6,2},{7,3},{8,12},{9,13},{10,... | collective-permute-start | bytes 1720328 | tf_op jit(solution)/shard_map/ppermute | solution.py:12
  37.3 18.0 %copy-start.1 = (bf16[1024,512]{1,0:T(8,128)(2,1)S(1)}, bf16[1024,512]{1,0:T(8,128)(2,1)}, u32[]{:S(2)}) copy-start(bf16[1024,512]{1,0:T(8,128)(2,1)} %param.8) | copy-start | bytes 3145732
  53.4 5.4 %collective-permute-start.3 = (f32[6,32,80]{2,1,0:T(8,128)S(1)}, f32[6,32,80]{2,1,0:T(8,128)S(1)}, u32[]{:S(2)}, u32[]{:S(2)}) collective-permute-start(f32[6,32,80]{2,1,0:T(8,128)S(1)} %dynamic-slice_add_fusion), channel_id=1, source_target_pairs={{0,8},{8,0},{16,24},{24,16},{32,40},{40,32},{48,56},{56,48},{64,72... | collective-permute-start | bytes 184328 | tf_op jit(solution)/shard_map/ppermute | solution.py:12
  55.3 2.6 %slice-start.2 = ((bf16[10,32,1024]{2,1,0:T(8,128)(2,1)}), bf16[1,32,1024]{2,1,0:T(8,128)(2,1)S(1)}, s32[]{:S(2)}) async-start(bf16[10,32,1024]{2,1,0:T(8,128)(2,1)} %param.10), calls=%async_computation.2 | async-start | bytes 131072 | tf_op jit(solution)/shard_map/slice | solution.py:96
  57.9 12.8 %copy-start.5 = (s32[10]{0:T(128)S(1)}, s32[10]{0:T(128)}, u32[]{:S(2)}) copy-start(s32[10]{0:T(128)} %param.11) | copy-start | bytes 124
  57.9 33.7 %slice-start.3 = ((bf16[10,32,1024]{2,1,0:T(8,128)(2,1)}), bf16[1,32,1024]{2,1,0:T(8,128)(2,1)S(1)}, s32[]{:S(2)}) async-start(bf16[10,32,1024]{2,1,0:T(8,128)(2,1)} %param.9), calls=%async_computation.3 | async-start | bytes 131072 | tf_op jit(solution)/shard_map/slice | solution.py:106
  58.7 7.0 %collective-permute-start.4 = (f32[5,32,80]{2,1,0:T(8,128)S(1)}, f32[5,32,80]{2,1,0:T(8,128)S(1)}, u32[]{:S(2)}, u32[]{:S(2)}) collective-permute-start(f32[5,32,80]{2,1,0:T(8,128)S(1)} %slice_add_fusion.2), channel_id=1, source_target_pairs={{0,16},{8,24},{16,0},{24,8},{32,48},{40,56},{48,32},{56,40},{64,80... | collective-permute-start | bytes 153608 | tf_op jit(solution)/shard_map/ppermute | solution.py:12
  65.7 10.3 %collective-permute-start.5 = (f32[4,32,80]{2,1,0:T(8,128)S(1)}, f32[4,32,80]{2,1,0:T(8,128)S(1)}, u32[]{:S(2)}, u32[]{:S(2)}) collective-permute-start(f32[4,32,80]{2,1,0:T(8,128)S(1)} %slice_add_fusion.3), channel_id=1, source_target_pairs={{0,32},{8,40},{16,48},{24,56},{32,0},{40,8},{48,16},{56,24},{64,96... | collective-permute-start | bytes 122888 | tf_op jit(solution)/shard_map/ppermute | solution.py:12
  76.0 13.5 %collective-permute-start.6 = (f32[3,32,80]{2,1,0:T(8,128)S(1)}, f32[3,32,80]{2,1,0:T(8,128)S(1)}, u32[]{:S(2)}, u32[]{:S(2)}) collective-permute-start(f32[3,32,80]{2,1,0:T(8,128)S(1)} %slice_add_fusion.4), channel_id=1, source_target_pairs={{0,64},{8,72},{16,80},{24,88},{32,96},{40,104},{48,112},{56,120},{... | collective-permute-start | bytes 92168 | tf_op jit(solution)/shard_map/ppermute | solution.py:12
  89.6 4.9 %collective-permute-start.7 = (f32[2,32,80]{2,1,0:T(8,128)S(1)}, f32[2,32,80]{2,1,0:T(8,128)S(1)}, u32[]{:S(2)}, u32[]{:S(2)}) collective-permute-start(f32[2,32,80]{2,1,0:T(8,128)S(1)} %slice_add_fusion.5), channel_id=1, source_target_pairs={{0,128},{8,136},{16,144},{24,152},{32,160},{40,168},{48,176},{56,1... | collective-permute-start | bytes 61448 | tf_op jit(solution)/shard_map/ppermute | solution.py:12
  94.5 12.7 %collective-permute-start.8 = (f32[1,32,80]{2,1,0:T(8,128)S(1)}, f32[1,32,80]{2,1,0:T(8,128)S(1)}, u32[]{:S(2)}, u32[]{:S(2)}) collective-permute-start(f32[1,32,80]{2,1,0:T(8,128)S(1)} %slice_add_fusion.6), channel_id=1, source_target_pairs={{0,256},{8,264},{16,272},{24,280},{32,288},{40,296},{48,304},{56,3... | collective-permute-start | bytes 30728 | tf_op jit(solution)/shard_map/ppermute | solution.py:12
  141.3 0.9 slice-start
  141.4 0.9 slice-start.1
where the time goes:
time: 156 us; the launch traced here: 154 us
  waiting for transfers between devices  49.2 us (32%)
  starting transfers between devices  37 us (24%)
  blocking collectives  33.9 us (22%)
  local copies, waits for them, and re-layouts  23.2 us (15%)
  matrix products  9.2 us (6%)
    ppermute x9, waiting for transfers between devices, partner(): lax.ppermute(x, axis, [(i, i ^ 1 << distance) for i in range(lax.axis_siz...  49.2 us
    ppermute x9, starting transfers between devices, partner(): lax.ppermute(x, axis, [(i, i ^ 1 << distance) for i in range(lax.axis_siz...  37 us
    all_gather x4, blocking collectives, stacked_from(): blocks = lax.all_gather(blocks, axes[k])  33.9 us
    scatter x1, local copies, waits for them, and re-layouts, per_device(): jnp.zeros_like(sources).at[local_index].set(result.astype(jnp.bfloat16))  6.79 us
    gather x1, local copies, waits for them, and re-layouts, per_device(): ordered = sources[local_index]  4.02 us
    dot_general x1, matrix products, per_device(): jnp.einsum('lkn,lkr->nr', u_factors[:dev_bits], far_coef, preferred_eleme...  3.67 us
    reshape x1, local copies, waits for them, and re-layouts, per_device(): result = jnp.einsum('gij,gjr->gir', leaf_blocks.reshape(leaf_count, leaf_...  3.25 us
    reshape x1, local copies, waits for them, and re-layouts, per_device(): result = result + jnp.einsum('kgs,gkr->gsr', u_factors[9].reshape(rank_ca...  3.23 us
  transfers between devices with their start and end apart: 9, of which 8 were waited for; matrix products, arithmetic and copies ran while one was open for 8% of the time, Pallas kernels for 0%

commit v1 on v0

v1 whole, which is shorter than its diff:
```python
import functools

import jax
import jax.numpy as jnp
from jax import lax
from jax.experimental import pallas as pl
from jax.experimental.pallas import tpu as pltpu
from jax.sharding import Mesh
from jax.sharding import PartitionSpec as P

AXES = ("y", "z", "x", "c")
MESH_ID = pl.DeviceIdType.MESH
NT = (((1,), (1,)), ((), ()))
TN = (((0,), (0,)), ((), ()))
NN = (((1,), (0,)), ((), ()))
F32 = jnp.float32
BF16 = jnp.bfloat16
RANK = 32
RHS = 640
ROWS = 1024
LEAF = 512
STEP = 128


def dot(a, b, dims=NN):
    return lax.dot_general(a, b, dims, preferred_element_type=F32)


def flip(v, mask):
    out, bit = v, 1
    while bit <= mask:
        if mask & bit:
            out = out + bit - 2 * bit * ((v // bit) % 2)
        bit *= 2
    return out


def kernel(
    perm_ref, ranks_ref, src_hbm, leaf_hbm, u_hbm, v_hbm, out_hbm,
    src, leaf, u, v, pt, vp, uperm, up_far, up_near, ordered, leaf_rows, near_far, acc, out,
    coef, core_in, twin_in, xs, xin, six, seven, pair_out, pair_in,
    n0, n1, n23, in0, in1, in23, four_in, five_in, fs, far_in, quad, quad_in, e0, e0_in, e1, e1_in,
    load_sem, out_sem, send_sem, recv_sem,
):
    y, z, x, c = (lax.axis_index(name) for name in AXES)
    zq = z % 4

    count = [0]
    started = []

    def target(dy=0, dz=0, dx=0, dc=0):
        return (flip(y, dy), flip(z, dz), flip(x, dx), flip(c, dc))

    def send(source, dest, **by):
        k = count[0]
        count[0] += 1
        copy = pltpu.make_async_remote_copy(
            src_ref=source, dst_ref=dest, send_sem=send_sem.at[k], recv_sem=recv_sem.at[k],
            device_id=target(**by), device_id_type=MESH_ID,
        )
        copy.start()
        started.append(copy)
        return copy

    loads = []
    for k, (a, b) in enumerate(((v_hbm, v), (src_hbm, src), (leaf_hbm, leaf), (u_hbm, u))):
        copy = pltpu.make_async_copy(a, b, load_sem.at[k])
        copy.start()
        loads.append(copy)

    partners = [dict(dc=1)]
    partners += [dict(dx=d, dc=e) for d in (1, 2, 3) for e in (0, 1)]
    partners += [dict(dy=a, dz=b) for a in range(4) for b in range(4) if a or b]
    partners += [dict(dz=d) for d in (4, 8, 12)]
    barrier = pltpu.get_barrier_semaphore()
    for by in partners:
        pl.semaphore_signal(barrier, inc=1, device_id=target(**by), device_id_type=MESH_ID)

    first_row = (((y * 16 + z) * 4 + x) * 2 + c) * ROWS
    local = perm_ref[...] - first_row

    def one_hot(k, _):
        rows = lax.broadcasted_iota(jnp.int32, (STEP, ROWS), 0) + k * STEP
        at = pl.ds(pl.multiple_of(k * STEP, STEP), STEP)
        pt[at, :] = jnp.where(rows == local, 1.0, 0.0).astype(BF16)
        return 0

    lax.fori_loop(0, ROWS // STEP, one_hot, 0)
    loads[0].wait()
    for k in range(4):
        at = slice(k * 256, k * 256 + 256)
        vp[:, at] = dot(v[0:288, :], pt[at, :], NT).astype(BF16)
    loads[1].wait()
    for n in range(5):
        cols = slice(n * 128, n * 128 + 128)
        coef[:, :, :, cols] = dot(vp[...], src[:, cols]).reshape(9, 2, 16, 128)

    pl.semaphore_wait(barrier, len(partners))

    core_a = send(coef.at[0:2, 1 - c], core_in.at[0:2], dc=1)
    core_b = send(coef.at[2:8, 1 - c], core_in.at[2:8], dc=1)
    twin = send(coef.at[8], twin_in, dc=1)

    def chip_sum(level):
        total = coef[level, c] + core_in[level]
        for q in range(4):
            xs[q, level] = total[4 * q : 4 * q + 4]

    core_a.wait_recv()
    for level in (0, 1):
        chip_sum(level)
    x_a = [send(xs.at[flip(x, d), 0:2], xin.at[d - 1, 0:2], dx=d) for d in (1, 2, 3)]
    core_b.wait_recv()
    for level in (2, 3, 4, 5):
        chip_sum(level)
    x_b = [send(xs.at[flip(x, d), 2:6], xin.at[d - 1, 2:6], dx=d) for d in (1, 2, 3)]
    for k in (0, 1):
        pair_out[k] = coef[6 + k, c] + core_in[6 + k]
    six_in = [send(pair_out.at[0], six.at[d - 2], dx=d) for d in (2, 3)]
    seven_in = send(pair_out.at[1], seven, dx=1)

    def row_sum(level):
        return ((xs[x, level] + xin[0, level]) + xin[1, level]) + xin[2, level]

    for copy in x_a:
        copy.wait_recv()
    for level, held in ((0, n0), (1, n1)):
        total = row_sum(level)
        for q in range(4):
            held[q] = total[q : q + 1]
    near = [send(n0.at[flip(zq, b)], in0.at[(a - 2) * 4 + b], dy=a, dz=b) for a in (2, 3) for b in range(4)]
    near += [send(n1.at[flip(zq, b)], in1.at[b], dy=1, dz=b) for b in range(4)]
    for copy in x_b:
        copy.wait_recv()
    for k, level in ((0, 2), (1, 3)):
        total = row_sum(level)
        for q in range(4):
            n23[q, k] = total[q : q + 1]
    near += [send(n23.at[flip(zq, b)], in23.at[b - 1], dz=b) for b in (1, 2, 3)]
    e1[0:4] = row_sum(4)
    e1[4:8] = row_sum(5)
    fours = [send(e1.at[0:4], four_in.at[d - 2], dz=d) for d in (2, 3)]
    fives = send(e1.at[4:8], five_in, dz=1)

    for copy in near:
        copy.wait_recv()
    total = in0[0]
    for k in range(1, 8):
        total = total + in0[k]
    fs[1] = total
    fs[2] = ((in1[0] + in1[1]) + in1[2]) + in1[3]
    for k, slot in ((0, 3), (1, 0)):
        fs[slot] = ((n23[zq, k] + in23[0, k]) + in23[1, k]) + in23[2, k]
    far = [send(fs.at[0:3], far_in.at[0], dz=4)]
    far += [send(fs.at[1:4], far_in.at[d], dz=4 + 4 * d) for d in (1, 2)]

    for copy in six_in:
        copy.wait_recv()
    seven_in.wait_recv()
    pair_in[0, 0] = six[0] + six[1]
    pair_in[0, 1] = seven[...]
    pair_copy = send(pair_in.at[0], pair_in.at[1], dc=1)
    for copy in fours:
        copy.wait_recv()
    fives.wait_recv()
    e1_in[0, 0:4] = four_in[0] + four_in[1]
    e1_in[0, 4:8] = five_in[...]
    shares = [(d, e) for d in range(4) for e in range(2) if d or e]
    e1_copies = [send(e1_in.at[0], e1_in.at[d * 2 + e], dx=d, dc=e) for d, e in shares]

    loads[2].wait()
    loads[3].wait()

    def ordered_step(k, _):
        at = pl.ds(pl.multiple_of(k * STEP, STEP), STEP)
        ordered[at, :] = dot(pt[:, at], src[...], TN).astype(BF16)
        return 0

    lax.fori_loop(0, ROWS // STEP, ordered_step, 0)

    def rank_rows(level, limit_shape):
        out_rank = jnp.zeros(limit_shape, jnp.int32)
        for k in range(10):
            out_rank = jnp.where(level == k, ranks_ref[k], out_rank)
        return out_rank

    shape = (288, 288)
    row = lax.broadcasted_iota(jnp.int32, shape, 0)
    col = lax.broadcasted_iota(jnp.int32, shape, 1)
    slot_a, inner_a = row >> 4, row & 15
    level_a = inner_a & 3
    k_a = 16 * (c ^ (slot_a & 1)) + 4 * (x ^ (slot_a >> 1)) + (zq ^ (inner_a >> 2))
    row_b = row - 128
    slot_b, inner_b = row_b >> 3, row_b & 7
    level_b = 4 + (inner_b >> 2)
    k_b = 16 * (c ^ (slot_b & 1)) + 4 * (x ^ (slot_b >> 1)) + (inner_b & 3)
    row_c = row - 192
    level_c = 6 + ((row_c >> 4) & 1)
    k_c = 16 * (c ^ (row_c >> 5)) + (row_c & 15)
    row_d = row - 256
    level = jnp.where(row < 128, level_a, jnp.where(row < 192, level_b, jnp.where(row < 256, level_c, 8)))
    k_of = jnp.where(row < 128, k_a, jnp.where(row < 192, k_b, jnp.where(row < 256, k_c, row_d)))
    keep = (col == level * RANK + k_of) & (k_of < rank_rows(level, shape))
    pick = jnp.where(keep, 1.0, 0.0).astype(BF16)
    for n in range(4):
        at = slice(n * 256, n * 256 + 256)
        uperm[0:288, at] = dot(pick, u[0:288, at]).astype(BF16)
    shape = (RANK, LEAF)
    live = lax.broadcasted_iota(jnp.int32, shape, 0) < ranks_ref[9]
    zeros = jnp.zeros(shape, BF16)
    uperm[288:320, 0:LEAF] = jnp.where(live, u[288:320, 0:LEAF], zeros)
    uperm[288:320, LEAF:] = zeros
    uperm[320:352, 0:LEAF] = zeros
    uperm[320:352, LEAF:] = jnp.where(live, u[288:320, LEAF:], zeros)

    def up_step(k, _):
        at = pl.ds(pl.multiple_of(k * STEP, STEP), STEP)
        up_far[at, :] = dot(pt[at, :], uperm[0:128, :], NT).astype(BF16)
        up_near[at, :] = dot(pt[at, :], uperm[128:352, :], NT).astype(BF16)
        for g in range(2):
            cols = slice(g * LEAF, g * LEAF + LEAF)
            leaf_rows[at, cols] = dot(pt[at, cols], leaf[cols, :]).astype(BF16)
        return 0

    lax.fori_loop(0, ROWS // STEP, up_step, 0)

    for g in range(2):
        other = slice((1 - g) * LEAF, (1 - g) * LEAF + LEAF)
        got = dot(v[288:320, other], ordered[other, :])
        near_far[160 + 32 * g : 192 + 32 * g, :] = got.astype(BF16)
    twin.wait_recv()
    near_far[128:160, :] = twin_in[...].reshape(32, RHS).astype(BF16)
    pair_copy.wait_recv()
    near_far[64:128, :] = pair_in[...].reshape(64, RHS).astype(BF16)
    for copy in e1_copies:
        copy.wait_recv()
    near_far[0:64, :] = e1_in[...].reshape(64, RHS).astype(BF16)

    def acc_step(k, _):
        at = pl.ds(pl.multiple_of(k * STEP, STEP), STEP)
        acc[at, :] = dot(leaf_rows[at, :], ordered[...]) + dot(up_near[at, :], near_far[...])
        return 0

    lax.fori_loop(0, ROWS // STEP, acc_step, 0)

    for copy in far:
        copy.wait_recv()
    quad[0] = ((fs[1] + far_in[0, 1]) + far_in[1, 0]) + far_in[2, 0]
    quad[1] = ((fs[2] + far_in[0, 2]) + far_in[1, 1]) + far_in[2, 1]
    quad[2] = far_in[1, 2] + far_in[2, 2]
    quad[3] = far_in[0, 0]
    quads = [send(quad, quad_in.at[b - 1], dz=b) for b in (1, 2, 3)]
    for k in range(4):
        e0[k : k + 1] = quad[k]
    for copy in quads:
        copy.wait_recv()
    for b in (1, 2, 3):
        for k in range(4):
            e0[4 * b + k : 4 * b + k + 1] = quad_in[b - 1, k]
    e0_copies = [send(e0, e0_in.at[d * 2 + e], dx=d, dc=e) for d, e in shares]
    e0_in[0] = e0[...]
    for copy in e0_copies:
        copy.wait_recv()
    far_rows = e0_in[...].reshape(128, RHS).astype(BF16)

    for k in range(ROWS // STEP):
        at = slice(k * STEP, k * STEP + STEP)
        out[at, :] = (acc[at, :] + dot(up_far[at, :], far_rows)).astype(BF16)
        pltpu.make_async_copy(out.at[at], out_hbm.at[at], out_sem.at[k]).start()
    for copy in started:
        copy.wait_send()
    for k in range(ROWS // STEP):
        at = slice(k * STEP, k * STEP + STEP)
        pltpu.make_async_copy(out.at[at], out_hbm.at[at], out_sem.at[k]).wait()


def per_device(sources, tree_perm, leaf_blocks, u_factors, v_factors, level_ranks):
    vmem = pltpu.VMEM
    copies = 80
    scratch = [
        vmem((ROWS, RHS), BF16), vmem((ROWS, LEAF), BF16), vmem((320, ROWS), BF16), vmem((320, ROWS), BF16),
        vmem((ROWS, ROWS), BF16), vmem((288, ROWS), BF16), vmem((352, ROWS), BF16),
        vmem((ROWS, 128), BF16), vmem((ROWS, 224), BF16), vmem((ROWS, RHS), BF16), vmem((ROWS, ROWS), BF16),
        vmem((224, RHS), BF16), vmem((ROWS, RHS), F32), vmem((ROWS, RHS), BF16),
        vmem((9, 2, 16, RHS), F32), vmem((8, 16, RHS), F32), vmem((2, 16, RHS), F32),
        vmem((4, 6, 4, RHS), F32), vmem((3, 6, 4, RHS), F32), vmem((2, 16, RHS), F32), vmem((16, RHS), F32),
        vmem((2, 16, RHS), F32), vmem((2, 2, 16, RHS), F32),
        vmem((4, 1, RHS), F32), vmem((4, 1, RHS), F32), vmem((4, 2, 1, RHS), F32),
        vmem((8, 1, RHS), F32), vmem((4, 1, RHS), F32), vmem((3, 2, 1, RHS), F32),
        vmem((2, 4, RHS), F32), vmem((4, RHS), F32), vmem((4, 1, RHS), F32), vmem((3, 3, 1, RHS), F32),
        vmem((4, 1, RHS), F32), vmem((3, 4, 1, RHS), F32), vmem((16, RHS), F32), vmem((8, 16, RHS), F32),
        vmem((8, RHS), F32), vmem((8, 8, RHS), F32),
        pltpu.SemaphoreType.DMA((4,)), pltpu.SemaphoreType.DMA((8,)),
        pltpu.SemaphoreType.DMA((copies,)), pltpu.SemaphoreType.DMA((copies,)),
    ]
    anywhere = pl.BlockSpec(memory_space=pl.ANY)
    return pl.pallas_call(
        kernel,
        out_shape=jax.ShapeDtypeStruct((ROWS, RHS), BF16),
        in_specs=[
            pl.BlockSpec(memory_space=pltpu.VMEM), pl.BlockSpec(memory_space=pltpu.SMEM),
            anywhere, anywhere, anywhere, anywhere,
        ],
        out_specs=anywhere,
        scratch_shapes=scratch,
        compiler_params=pltpu.CompilerParams(
            collective_id=0, has_side_effects=True, vmem_limit_bytes=60 * 1024 * 1024
        ),
    )(
        tree_perm.reshape(1, ROWS), level_ranks, sources, leaf_blocks,
        u_factors.reshape(320, ROWS), v_factors.reshape(320, ROWS),
    )


def solution(mesh):
    torus = Mesh(mesh.devices.reshape(4, 16, 4, 2), AXES)
    placed = (P(AXES, None), P(AXES), P(AXES, None), P(None, None, AXES), P(None, None, AXES), P())
    return jax.shard_map(per_device, mesh=torus, in_specs=placed, out_specs=P(AXES, None), check_vma=False)
```

time: 156 us -> 53.6 us (0.34); the launches traced: 154 us -> 53.4 us
  Pallas kernels: 0 us -> 50.9 us
  waiting for transfers between devices: 49.2 us -> 0 us
  starting transfers between devices: 37 us -> 0 us
  blocking collectives: 33.9 us -> 0 us
  local copies, waits for them, and re-layouts: 23.2 us -> 2.49 us
  matrix products: 9.2 us -> 0 us
    pallas_call x0 -> x1, Pallas kernels: none -> 50.9 us  [per_device(): pl.pallas_call(kernel, out_shape=jax.ShapeDtypeStruct((ROWS, RHS), BF16),...]
    ppermute x9 -> x0, waiting for transfers between devices: 49.2 us -> none  [partner(): lax.ppermute(x, axis, [(i, i ^ 1 << distance) for i in range(lax.axis_siz...]
    ppermute x9 -> x0, starting transfers between devices: 37 us -> none  [partner(): lax.ppermute(x, axis, [(i, i ^ 1 << distance) for i in range(lax.axis_siz...]
    all_gather x4 -> x0, blocking collectives: 33.9 us -> none  [stacked_from(): blocks = lax.all_gather(blocks, axes[k])]
    dot_general x5 -> x0, matrix products: 9.2 us -> none  [the longest x1 3.67 us: per_device(): jnp.einsum('lkn,lkr->nr', u_factors[:dev_bits], far_coef, preferred_eleme...]
    scatter x1 -> x0, local copies, waits for them, and re-layouts: 6.79 us -> none  [per_device(): jnp.zeros_like(sources).at[local_index].set(result.astype(jnp.bfloat16))]
    reshape x3 -> x0, local copies, waits for them, and re-layouts: 6.73 us -> none  [the longest x1 3.25 us: per_device(): result = jnp.einsum('gij,gjr->gir', leaf_blocks.reshape(leaf_count, leaf_...]
    gather x1 -> x0, local copies, waits for them, and re-layouts: 4.02 us -> none  [per_device(): ordered = sources[local_index]]
  transfers between devices with their start and end apart: 9 -> 0, of which waited for: 8 -> 0; matrix products, arithmetic and copies ran while one was open for 8% -> 0% of each run, Pallas kernels for 0% -> 0%
where the time goes in v1:
time: 53.6 us; the launch traced here: 53.4 us
  Pallas kernels  50.9 us (95%)
  local copies, waits for them, and re-layouts  2.49 us (5%)
    pallas_call x1, Pallas kernels, per_device(): pl.pallas_call(kernel, out_shape=jax.ShapeDtypeStruct((ROWS, RHS), BF16),...  50.9 us
    unnamed x1, local copies, waits for them, and re-layouts  2.49 us

profile of v1, /device:TPU:1, one launch (start us, length us, event | category | flops | bytes accessed | tf_op | source)
XLA Modules:
  0.0 53.4 jit_solution(6577237188432348114)
XLA Ops:
  0.0 50.9 %shard_map.64 = bf16[1024,640]{1,0:T(8,128)(2,1)} custom-call(s32[1,1024]{1,0:T(1,128)} %bitcast.5, s32[10]{0:T(128)} %ranks_ref.1, bf16[1024,640]{1,0:T(8,128)(2,1)} %src_hbm.1, bf16[1024,512]{1,0:T(8,128)(2,1)} %leaf_hbm.1, bf16[320,1024]{1,0:T(8,128)(2,1)} %bitcast.3, bf16[320,1024]{1,0:T(8,128)(2,1)} %bitcast.4), custom_call_target="tpu_custom_call" | custom-call | tf_op jit(solution)/shard_map/pallas_call | solution.py:297
  50.9 2.5 %copy.8 = bf16[1024,640]{1,0:T(8,128)(2,1)} copy(bf16[1024,640]{1,0:T(8,128)(2,1)} %shard_map.64) | data formatting | bytes 2621440

commit v2 on v1

v2 whole, which is shorter than its diff:
```python
import functools

import jax
import jax.numpy as jnp
from jax import lax
from jax.experimental import pallas as pl
from jax.experimental.pallas import tpu as pltpu
from jax.sharding import Mesh
from jax.sharding import PartitionSpec as P

AXES = ("y", "z", "x", "c")
MESH_ID = pl.DeviceIdType.MESH
NT = (((1,), (1,)), ((), ()))
TN = (((0,), (0,)), ((), ()))
NN = (((1,), (0,)), ((), ()))
F32 = jnp.float32
BF16 = jnp.bfloat16
RANK = 32
RHS = 640
ROWS = 1024
LEAF = 512
STEP = 128
BLOCK = 256


def dot(a, b, dims=NN):
    return lax.dot_general(a, b, dims, preferred_element_type=F32)


def flip(v, mask):
    out, bit = v, 1
    while bit <= mask:
        if mask & bit:
            out = out + bit - 2 * bit * ((v // bit) % 2)
        bit *= 2
    return out


def kernel(
    perm_hbm, ranks_ref, src_hbm, leaf_hbm, u_hbm, v_hbm, acc, up_far, far_rows,
    perm, src, leaf, u, v, pt, vp, uperm, up_near, ordered, leaf_rows, near_far,
    coef, core_in, twin_in, xs, xin, six, seven, pair_out, pair_in,
    n0, n1, n23, in0, in1, in23, four_in, five_in, fs, far_in, quad, quad_in, e0_in, e1, e1_in,
    load_sem, send_sem, recv_sem,
):
    y, z, x, c = (lax.axis_index(name) for name in AXES)
    zq = z % 4

    count = [0]
    started = []

    def target(dy=0, dz=0, dx=0, dc=0):
        return (flip(y, dy), flip(z, dz), flip(x, dx), flip(c, dc))

    def send(source, dest, **by):
        k = count[0]
        count[0] += 1
        copy = pltpu.make_async_remote_copy(
            src_ref=source, dst_ref=dest, send_sem=send_sem.at[k], recv_sem=recv_sem.at[k],
            device_id=target(**by), device_id_type=MESH_ID,
        )
        copy.start()
        started.append(copy)
        return copy

    partners = [dict(dc=1)]
    partners += [dict(dx=d) for d in (1, 2, 3)]
    partners += [dict(dy=a, dz=b) for a in range(4) for b in range(4) if a or b]
    partners += [dict(dz=d) for d in (4, 8, 12)]
    barrier = pltpu.get_barrier_semaphore()
    for by in partners:
        pl.semaphore_signal(barrier, inc=1, device_id=target(**by), device_id_type=MESH_ID)

    loads = []

    def load(a, b):
        copy = pltpu.make_async_copy(a, b, load_sem.at[len(loads)])
        copy.start()
        loads.append(copy)
        return copy

    perm_load = load(perm_hbm, perm)
    v_first = load(v_hbm.at[0:128], v.at[0:128])
    src_loads = [load(src_hbm.at[k : k + 256], src.at[k : k + 256]) for k in range(0, ROWS, 256)]
    v_rest = load(v_hbm.at[128:320], v.at[128:320])

    first_row = (((y * 16 + z) * 4 + x) * 2 + c) * ROWS
    perm_load.wait()
    local = perm[...] - first_row

    def one_hot(k, _):
        rows = lax.broadcasted_iota(jnp.int32, (STEP, ROWS), 0) + k * STEP
        at = pl.ds(pl.multiple_of(k * STEP, STEP), STEP)
        pt[at, :] = jnp.where(rows == local, 1.0, 0.0).astype(BF16)
        return 0

    lax.fori_loop(0, ROWS // STEP, one_hot, 0)
    v_first.wait()
    for k in range(4):
        at = slice(k * 256, k * 256 + 256)
        vp[0:128, at] = dot(v[0:128, :], pt[at, :], NT).astype(BF16)
    for copy in src_loads:
        copy.wait()
    for n in range(0, RHS, 128):
        cols = slice(n, n + 128)
        coef[0:4, :, :, cols] = dot(vp[0:128, :], src[:, cols]).reshape(4, 2, 16, 128)
    leaf_load = load(leaf_hbm, leaf)
    u_load = load(u_hbm, u)

    def order_rows():
        u_load.wait()

        def ordered_step(k, _):
            at = pl.ds(pl.multiple_of(k * BLOCK, BLOCK), BLOCK)
            ordered[at, :] = dot(pt[:, at], src[...], TN).astype(BF16)
            return 0

        lax.fori_loop(0, ROWS // BLOCK, ordered_step, 0)

        shape = (288, 288)
        row = lax.broadcasted_iota(jnp.int32, shape, 0)
        col = lax.broadcasted_iota(jnp.int32, shape, 1)
        slot_a, inner_a = row >> 4, row & 15
        level_a = inner_a & 3
        k_a = 16 * (c ^ (slot_a & 1)) + 4 * (x ^ (slot_a >> 1)) + (zq ^ (inner_a >> 2))
        row_b = row - 128
        slot_b, inner_b = row_b >> 3, row_b & 7
        level_b = 4 + (inner_b >> 2)
        k_b = 16 * (c ^ (slot_b & 1)) + 4 * (x ^ (slot_b >> 1)) + (inner_b & 3)
        row_c = row - 192
        level_c = 6 + ((row_c >> 4) & 1)
        k_c = 16 * (c ^ (row_c >> 5)) + (row_c & 15)
        row_d = row - 256

        def by_part(parts):
            return jnp.where(row < 128, parts[0], jnp.where(row < 192, parts[1], jnp.where(row < 256, parts[2], parts[3])))

        level = by_part((level_a, level_b, level_c, 8))
        k_of = by_part((k_a, k_b, k_c, row_d))
        limit = jnp.zeros(shape, jnp.int32)
        for k in range(9):
            limit = jnp.where(level == k, ranks_ref[k], limit)
        keep = (col == level * RANK + k_of) & (k_of < limit)
        pick = jnp.where(keep, 1.0, 0.0).astype(BF16)
        for n in range(4):
            at = slice(n * 256, n * 256 + 256)
            uperm[0:288, at] = dot(pick, u[0:288, at]).astype(BF16)
        shape = (RANK, LEAF)
        live = lax.broadcasted_iota(jnp.int32, shape, 0) < ranks_ref[9]
        zeros = jnp.zeros(shape, BF16)
        uperm[288:320, 0:LEAF] = jnp.where(live, u[288:320, 0:LEAF], zeros)
        uperm[288:320, LEAF:] = zeros
        uperm[320:352, 0:LEAF] = zeros
        uperm[320:352, LEAF:] = jnp.where(live, u[288:320, LEAF:], zeros)

    def local_dots():
        leaf_load.wait()

        def up_step(k, _):
            at = pl.ds(pl.multiple_of(k * BLOCK, BLOCK), BLOCK)
            up_far[at, :] = dot(pt[at, :], uperm[0:128, :], NT).astype(BF16)
            up_near[at, :] = dot(pt[at, :], uperm[128:352, :], NT).astype(BF16)
            for g in range(2):
                cols = slice(g * LEAF, g * LEAF + LEAF)
                leaf_rows[at, cols] = dot(pt[at, cols], leaf[cols, :]).astype(BF16)
            return 0

        lax.fori_loop(0, ROWS // BLOCK, up_step, 0)

        def leaf_step(k, _):
            at = pl.ds(pl.multiple_of(k * BLOCK, BLOCK), BLOCK)
            acc[at, :] = dot(leaf_rows[at, :], ordered[...])
            return 0

        lax.fori_loop(0, ROWS // BLOCK, leaf_step, 0)

    pl.when(z < 8)(order_rows)
    pl.when(z < 4)(local_dots)

    pl.semaphore_wait(barrier, len(partners))

    core_a = [send(coef.at[k : k + 2, 1 - c], core_in.at[k : k + 2], dc=1) for k in (0, 2)]
    v_rest.wait()
    for k in range(4):
        at = slice(k * 256, k * 256 + 256)
        vp[128:288, at] = dot(v[128:288, :], pt[at, :], NT).astype(BF16)
    for n in range(0, RHS, 128):
        cols = slice(n, n + 128)
        coef[4:9, :, :, cols] = dot(vp[128:288, :], src[:, cols]).reshape(5, 2, 16, 128)

    def chip_sum(level):
        total = coef[level, c] + core_in[level]
        for q in range(4):
            xs[q, level] = total[4 * q : 4 * q + 4]

    def scatter_x(first):
        chip_sum(first)
        chip_sum(first + 1)
        return [send(xs.at[flip(x, d), first : first + 2], xin.at[d - 1, first : first + 2], dx=d) for d in (1, 2, 3)]

    def row_sum(level):
        return ((xs[x, level] + xin[0, level]) + xin[1, level]) + xin[2, level]

    core_a[0].wait_recv()
    x_a = scatter_x(0)
    core_a[1].wait_recv()
    x_b = scatter_x(2)
    core_b = send(coef.at[4:8, 1 - c], core_in.at[4:8], dc=1)
    twin = send(coef.at[8], twin_in, dc=1)

    for copy in x_a:
        copy.wait_recv()
    for level, held in ((0, n0), (1, n1)):
        total = row_sum(level)
        for q in range(4):
            held[q] = total[q : q + 1]
    near = [send(n0.at[flip(zq, b)], in0.at[(a - 2) * 4 + b], dy=a, dz=b) for a in (2, 3) for b in range(4)]
    near += [send(n1.at[flip(zq, b)], in1.at[b], dy=1, dz=b) for b in range(4)]
    for copy in x_b:
        copy.wait_recv()
    for k, level in ((0, 2), (1, 3)):
        total = row_sum(level)
        for q in range(4):
            n23[q, k] = total[q : q + 1]
    near += [send(n23.at[flip(zq, b)], in23.at[b - 1], dz=b) for b in (1, 2, 3)]

    core_b.wait_recv()
    x_c = scatter_x(4)
    for k in (0, 1):
        pair_out[k] = coef[6 + k, c] + core_in[6 + k]
    six_in = [send(pair_out.at[0], six.at[d - 2], dx=d) for d in (2, 3)]
    seven_in = send(pair_out.at[1], seven, dx=1)

    for copy in near:
        copy.wait_recv()
    total = in0[0]
    for k in range(1, 8):
        total = total + in0[k]
    fs[1] = total
    fs[2] = ((in1[0] + in1[1]) + in1[2]) + in1[3]
    for k, slot in ((0, 3), (1, 0)):
        fs[slot] = ((n23[zq, k] + in23[0, k]) + in23[1, k]) + in23[2, k]
    far = [send(fs.at[1:4], far_in.at[d], dz=4 + 4 * d) for d in (1, 2)]
    far += [send(fs.at[0:3], far_in.at[0], dz=4)]

    for copy in x_c:
        copy.wait_recv()
    e1[0:4] = row_sum(4)
    e1[4:8] = row_sum(5)
    fours = [send(e1.at[0:4], four_in.at[d - 2], dz=d) for d in (2, 3)]
    fives = send(e1.at[4:8], five_in, dz=1)
    for copy in six_in:
        copy.wait_recv()
    seven_in.wait_recv()
    pair_in[0, 0] = six[0] + six[1]
    pair_in[0, 1] = seven[...]
    pair_copy = send(pair_in.at[0], pair_in.at[1], dc=1)
    for copy in fours:
        copy.wait_recv()
    fives.wait_recv()
    e1_in[0, 0:4] = four_in[0] + four_in[1]
    e1_in[0, 4:8] = five_in[...]

    def share(held):
        to_twin = [send(held.at[0], held.at[1], dc=1)]
        across = [send(held.at[0], held.at[2 * d], dx=d) for d in (1, 3, 2)]
        return to_twin, across

    def relay(held, parts):
        to_twin, across = parts
        for copy, d in zip(across, (1, 3, 2)):
            copy.wait_recv()
            to_twin.append(send(held.at[2 * d], held.at[2 * d + 1], dc=1))
        for copy in to_twin:
            copy.wait_recv()

    e1_parts = share(e1_in)
    pl.when(z >= 8)(order_rows)
    pl.when(z >= 4)(local_dots)

    for copy in far:
        copy.wait_recv()
    quad[0] = ((fs[1] + far_in[0, 1]) + far_in[1, 0]) + far_in[2, 0]
    quad[1] = ((fs[2] + far_in[0, 2]) + far_in[1, 1]) + far_in[2, 1]
    quad[2] = far_in[1, 2] + far_in[2, 2]
    quad[3] = far_in[0, 0]
    quads = [send(quad, quad_in.at[b - 1], dz=b) for b in (3, 2, 1)]
    relay(e1_in, e1_parts)
    for k in range(4):
        e0_in[0, k : k + 1] = quad[k]
    for copy in quads:
        copy.wait_recv()
    for b in (1, 2, 3):
        for k in range(4):
            e0_in[0, 4 * b + k : 4 * b + k + 1] = quad_in[b - 1, k]
    e0_parts = share(e0_in)

    for g in range(2):
        other = slice((1 - g) * LEAF, (1 - g) * LEAF + LEAF)
        got = dot(v[288:320, other], ordered[other, :])
        near_far[160 + 32 * g : 192 + 32 * g, :] = got.astype(BF16)
    twin.wait_recv()
    near_far[128:160, :] = twin_in[...].reshape(32, RHS).astype(BF16)
    pair_copy.wait_recv()
    near_far[64:128, :] = pair_in[...].reshape(64, RHS).astype(BF16)
    near_far[0:64, :] = e1_in[...].reshape(64, RHS).astype(BF16)

    def acc_step(k, _):
        at = pl.ds(pl.multiple_of(k * BLOCK, BLOCK), BLOCK)
        acc[at, :] = acc[at, :] + dot(up_near[at, :], near_far[...])
        return 0

    lax.fori_loop(0, ROWS // BLOCK, acc_step, 0)

    relay(e0_in, e0_parts)
    far_rows[...] = e0_in[...].reshape(128, RHS).astype(BF16)
    for copy in started:
        copy.wait_send()


def last(acc, up_far, far_rows, out_hbm, out, out_sem):
    copies = []
    for k in range(ROWS // STEP):
        at = slice(k * STEP, k * STEP + STEP)
        out[at, :] = (acc[at, :] + dot(up_far[at, :], far_rows[...])).astype(BF16)
        copies.append(pltpu.make_async_copy(out.at[at], out_hbm.at[at], out_sem.at[k]))
        copies[-1].start()
    for copy in copies:
        copy.wait()


def per_device(sources, tree_perm, leaf_blocks, u_factors, v_factors, level_ranks):
    vmem = pltpu.VMEM
    copies = 64
    scratch = [
        vmem((1, ROWS), jnp.int32),
        vmem((ROWS, RHS), BF16), vmem((ROWS, LEAF), BF16), vmem((320, ROWS), BF16), vmem((320, ROWS), BF16),
        vmem((ROWS, ROWS), BF16), vmem((288, ROWS), BF16), vmem((352, ROWS), BF16),
        vmem((ROWS, 224), BF16), vmem((ROWS, RHS), BF16), vmem((ROWS, ROWS), BF16), vmem((224, RHS), BF16),
        vmem((9, 2, 16, RHS), F32), vmem((8, 16, RHS), F32), vmem((2, 16, RHS), F32),
        vmem((4, 6, 4, RHS), F32), vmem((3, 6, 4, RHS), F32), vmem((2, 16, RHS), F32), vmem((16, RHS), F32),
        vmem((2, 16, RHS), F32), vmem((2, 2, 16, RHS), F32),
        vmem((4, 1, RHS), F32), vmem((4, 1, RHS), F32), vmem((4, 2, 1, RHS), F32),
        vmem((8, 1, RHS), F32), vmem((4, 1, RHS), F32), vmem((3, 2, 1, RHS), F32),
        vmem((2, 4, RHS), F32), vmem((4, RHS), F32), vmem((4, 1, RHS), F32), vmem((3, 3, 1, RHS), F32),
        vmem((4, 1, RHS), F32), vmem((3, 4, 1, RHS), F32), vmem((8, 16, RHS), F32),
        vmem((8, RHS), F32), vmem((8, 8, RHS), F32),
        pltpu.SemaphoreType.DMA((9,)), pltpu.SemaphoreType.DMA((copies,)), pltpu.SemaphoreType.DMA((copies,)),
    ]
    anywhere = pl.BlockSpec(memory_space=pltpu.HBM)
    inside = pl.BlockSpec(memory_space=vmem)
    held = pl.pallas_call(
        kernel,
        out_shape=(vmem((ROWS, RHS), F32), vmem((ROWS, 128), BF16), vmem((128, RHS), BF16)),
        in_specs=[anywhere, pl.BlockSpec(memory_space=pltpu.SMEM), anywhere, anywhere, anywhere, anywhere],
        out_specs=(inside, inside, inside),
        scratch_shapes=scratch,
        compiler_params=pltpu.CompilerParams(
            collective_id=0, has_side_effects=True, vmem_limit_bytes=63_800_000
        ),
    )(
        tree_perm.reshape(1, ROWS), level_ranks, sources, leaf_blocks,
        u_factors.reshape(320, ROWS), v_factors.reshape(320, ROWS),
    )
    held = [pltpu.with_memory_space_constraint(a, vmem) for a in held]
    return pl.pallas_call(
        last,
        out_shape=jax.ShapeDtypeStruct((ROWS, RHS), BF16),
        in_specs=[inside, inside, inside],
        out_specs=anywhere,
        scratch_shapes=[vmem((ROWS, RHS), BF16), pltpu.SemaphoreType.DMA((ROWS // STEP,))],
        compiler_params=pltpu.CompilerParams(vmem_limit_bytes=16 * 1024 * 1024),
    )(*held)


def solution(mesh):
    torus = Mesh(mesh.devices.reshape(4, 16, 4, 2), AXES)
    placed = (P(AXES, None), P(AXES), P(AXES, None), P(None, None, AXES), P(None, None, AXES), P())
    return jax.shard_map(per_device, mesh=torus, in_specs=placed, out_specs=P(AXES, None), check_vma=False)
```

time: 53.6 us -> 45.4 us (0.85)
  Pallas kernels: 50.9 us -> 45.2 us
  local copies, waits for them, and re-layouts: 2.49 us -> 0 us
    pallas_call x1 -> x2, Pallas kernels: 50.9 us -> 45.2 us  [the longest x1 43.9 us: per_device(): pl.pallas_call(kernel, out_shape=(vmem((ROWS, RHS), F32), vmem((ROWS, 128...]
    unnamed x1 -> x0, local copies, waits for them, and re-layouts: 2.49 us -> none
where the time goes in v2:
time: 45.4 us; the launch traced here: 45.2 us
  Pallas kernels  45.2 us (100%)
    pallas_call x1, Pallas kernels, per_device(): pl.pallas_call(kernel, out_shape=(vmem((ROWS, RHS), F32), vmem((ROWS, 128...  43.9 us
    pallas_call x1, Pallas kernels, per_device(): pl.pallas_call(last, out_shape=jax.ShapeDtypeStruct((ROWS, RHS), BF16), i...  1.32 us

profile of v2, /device:TPU:1, one launch (start us, length us, event | category | flops | bytes accessed | tf_op | source)
XLA Modules:
  0.0 45.2 jit_solution(8909806914981396258)
XLA Ops:
  0.0 43.9 %shard_map.64 = (f32[1024,640]{1,0:T(8,128)S(1)}, bf16[1024,128]{1,0:T(8,128)(2,1)S(1)}, bf16[128,640]{1,0:T(8,128)(2,1)S(1)}) custom-call(s32[1,1024]{1,0:T(1,128)} %bitcast.5, s32[10]{0:T(128)} %ranks_ref.1, bf16[1024,640]{1,0:T(8,128)(2,1)} %src_hbm.1, bf16[1024,512]{1,0:T(8,128)(2,1)} %leaf_hbm.1, bf16[320,1024]{1,0:T(8,128)(2,1)} %bitcast.3, ...), custom_call_target="tpu_custom_call" | custom-call | tf_op jit(solution)/shard_map/pallas_call | solution.py:352
  43.9 1.3 %shard_map.65 = bf16[1024,640]{1,0:T(8,128)(2,1)} custom-call(f32[1024,640]{1,0:T(8,128)S(1)} %get-tuple-element.8.acc, bf16[1024,128]{1,0:T(8,128)(2,1)S(1)} %get-tuple-element.9.up_far, bf16[128,640]{1,0:T(8,128)(2,1)S(1)} %get-tuple-element.10.far_rows), custom_call_target="tpu_custom_call" | custom-call | tf_op jit(solution)/shard_map/pallas_call | solution.py:366
